TPU v7x, 32 devices: a whole 2x2x4 slice. The times are simulated.
32 devices in a mesh: dp: 4 (over x, core), seq: 4 (over z), tensor: 2 (over y).
Axes of the slice: x: 2, y: 2, z: 4, core: 2. Of those that a mesh axis runs over, the one named last changes fastest.
Arguments:
- vit_out: bfloat16 [4096, 3200], P(('dp', 'seq')), may hold values from -6 to 6
- ln_gain: float32 [3200], replicated, may hold values from 0.1 to 1.9
- ln_bias: float32 [3200], replicated, may hold values from -3 to 3
- proj_weight: bfloat16 [3200, 4, 2048], P(None, None, 'tensor'), may hold values from -0.109375 to 0.109375
- proj_bias: float32 [4, 2048], P(None, 'tensor'), may hold values from -3 to 3
- text_embed: bfloat16 [16384, 8192], P('dp', ('seq', 'tensor')), may hold values from -6 to 6
- norm_gain: float32 [8192], P(('seq', 'tensor')), may hold values from 0.1 to 1.9
- tile_dest: int32 [32, 1], replicated, may hold values from 0 to 3; in each aligned block of 8 rows (0 to 7, 8 to 15, ...) at most 4 rows name the same one
- tile_place: int32 [4, 32], replicated, may hold values from 0 to 31, each once within a row
Outputs:
- normed: bfloat16 [16384, 8192], P('dp', ('seq', 'tensor'))
Inputs may be any that keep to these rules, and one draw needn't show every extreme that they name: `tile_dest`: in each aligned block of 8 rows (one encoder group's tiles) no replica is named more than 4 times, a bound that some block reaches. `tile_place`: each row is a permutation of 0 to 31.
All inputs are finite; a program needn't handle non-finite values.
Results may differ from a plain program's by a relative error of at most 0.0048.
Values may be sent and summed in bfloat16 or wider, within the bound.
A program may use at most 128 MiB of HBM per device.

v0:
```python
import jax
import jax.numpy as jnp
from jax import lax
from jax.sharding import PartitionSpec as P

D = 8192
TILE = 128


def layer_norm(rows, ln_gain, ln_bias):
    values = rows.astype(jnp.float32)
    center = values - jnp.mean(values, axis=-1, keepdims=True)
    spread = jnp.mean(center * center, axis=-1, keepdims=True)
    return (center * lax.rsqrt(spread + 1e-06) * ln_gain + ln_bias).astype(jnp.bfloat16)


def arrival_ranks(destination, replicas):
    onehot = (destination[:, None] == jnp.arange(replicas, dtype=jnp.int32)[None, :]).astype(
        jnp.int32
    )
    before = jnp.cumsum(onehot, axis=0) - onehot
    return jnp.sum(before * onehot, axis=1)


def row_squares(rows):
    values = rows.astype(jnp.float32)
    return jnp.sum(values * values, axis=-1)


def local(
    vit_out, ln_gain, ln_bias, proj_weight, proj_bias, text_embed, norm_gain, tile_dest, tile_place
):
    replicas = lax.axis_size("dp")
    owners = lax.axis_size("seq")
    my_replica = lax.axis_index("dp")
    local_rows = vit_out.shape[0]
    width_in = vit_out.shape[1]
    column_block = proj_weight.shape[2]
    positions = tile_place.shape[1]
    seq_rows = text_embed.shape[0]
    group_tiles = owners * local_rows // TILE
    total_tiles = tile_dest.shape[0]
    normed_in = layer_norm(vit_out, ln_gain, ln_bias)
    weights_flat = proj_weight.reshape(width_in, owners * column_block)
    hidden = jnp.dot(
        normed_in, weights_flat, preferred_element_type=jnp.float32
    ) + proj_bias.reshape(-1)
    projected = hidden.astype(jnp.bfloat16)
    regrouped = lax.all_to_all(
        projected.reshape(local_rows, owners, column_block),
        "seq",
        split_axis=1,
        concat_axis=0,
        tiled=True,
    )
    group_rows = regrouped.reshape(owners * local_rows, column_block)
    destination = tile_dest[:, 0]
    ranks = arrival_ranks(destination, replicas)
    place_row = lax.dynamic_index_in_dim(tile_place, my_replica, 0, keepdims=False)
    slot_of_tile = jnp.where(
        destination == my_replica, jnp.take(place_row, jnp.minimum(ranks, positions - 1)), -1
    )
    matches = slot_of_tile[None, :] == jnp.arange(positions, dtype=jnp.int32)[:, None]
    source_tile = (
        jnp.sum(
            matches.astype(jnp.int32) * (jnp.arange(total_tiles, dtype=jnp.int32) + 1)[None, :],
            axis=1,
        )
        - 1
    )
    text_tiles = text_embed.reshape(positions, TILE, column_block)
    capacity = max(2, 2 * group_tiles // replicas)
    local_dest = lax.dynamic_slice_in_dim(destination, my_replica * group_tiles, group_tiles)
    local_rank = arrival_ranks(local_dest, replicas)
    slot_index = local_dest * capacity + local_rank
    filling = slot_index[None, :] == jnp.arange(replicas * capacity, dtype=jnp.int32)[:, None]
    slot_source = (
        jnp.sum(
            filling.astype(jnp.int32) * (jnp.arange(group_tiles, dtype=jnp.int32) + 1)[None, :],
            axis=1,
        )
        - 1
    )
    tiles = group_rows.reshape(group_tiles, TILE, column_block)
    outgoing = jnp.where(
        (slot_source >= 0)[:, None, None],
        tiles[jnp.clip(slot_source, 0, group_tiles - 1)],
        jnp.zeros((), jnp.bfloat16),
    )
    outgoing = outgoing.reshape(replicas, capacity, TILE, column_block)
    incoming = lax.all_to_all(outgoing, "dp", split_axis=0, concat_axis=0, tiled=True).reshape(
        replicas * capacity, TILE, column_block
    )
    group_ranks = jax.vmap(lambda block: arrival_ranks(block, replicas))(
        destination.reshape(replicas, group_tiles)
    ).reshape(-1)
    safe_tile = jnp.clip(source_tile, 0, total_tiles - 1)
    arrival_index = safe_tile // group_tiles * capacity + jnp.take(group_ranks, safe_tile)
    picked = incoming[jnp.clip(arrival_index, 0, replicas * capacity - 1)]
    assembled = jnp.where((source_tile >= 0)[:, None, None], picked, text_tiles).reshape(
        seq_rows, column_block
    )
    squares = row_squares(assembled)
    totals = lax.psum(squares, ("seq", "tensor"))
    scale = lax.rsqrt(totals / D + 1e-05)
    return (assembled.astype(jnp.float32) * scale[:, None] * norm_gain).astype(jnp.bfloat16)


def solution(mesh):
    placed = (
        P(("dp", "seq"), None),
        P(),
        P(),
        P(None, None, "tensor"),
        P(None, "tensor"),
        P("dp", ("seq", "tensor")),
        P(("seq", "tensor")),
        P(),
        P(),
    )
    return jax.shard_map(
        local, mesh=mesh, in_specs=placed, out_specs=P("dp", ("seq", "tensor")), check_vma=False
    )
```

profile of v0, /device:TPU:0, one launch (start us, length us, event | category | flops | bytes accessed | tf_op | source)
XLA Modules:
  0.0 208.5 jit_solution(405158420390305600)
XLA Ops:
  0.0 0.0 copy-start
  0.0 0.0 copy-start.2
  0.0 0.0 copy-start.1
  0.0 0.0 copy-start.5
  0.0 0.0 copy-start.6
  0.0 18.2 %copy.13 = bf16[400,8,4,1024]{3,1,2,0:T(8,128)(2,1)} copy(bf16[400,8,4,1024]{3,2,1,0:T(4,128)(2,1)} %bitcast.39) | data formatting | bytes 52428800
  18.2 0.0 copy-done.2
  18.2 0.0 copy-done.1
  18.3 0.3 convert_reduce_fusion
  18.6 0.6 fusion.6
  19.2 0.0 copy-done.5
  19.2 0.0 copy-done.6
  19.2 12.3 %fusion.3 = bf16[256,4096]{1,0:T(8,128)(2,1)S(1)} fusion(bf16[3200,4096]{1,0:T(8,128)(2,1)} %bitcast.40, f32[4096]{0:T(1024)S(1)} %bitcast.46, bf16[256,3200]{1,0:T(8,128)(2,1)S(1)} %copy-done.1, f32[3200]{0:T(1024)S(1)} %copy-done.5, f32[3200]{0:T(1024)S(1)} %copy-done.6, f32[256]{0:T(256)S(1)} %add_rsqrt_fusion.1, f32[256]{0:T(256)S(1)} %broadcast_multiply_fusion), kind=kOutput, calls=%fused_computation.11 | convolution fusion | flops 6717898752 | bytes 29993984 | tf_op jit(solution)/shard_map/dot_general | solution.py:45
  31.5 0.0 copy-start.3
  31.5 1.5 copy.17
  33.0 6.4 %all-to-all-start = ((bf16[256,4,1024]{2,0,1:T(8,128)(2,1)}), bf16[256,4,1024]{2,0,1:T(8,128)(2,1)S(1)}, u32[]{:S(2)}, u32[]{:S(2)}) async-start(bf16[256,4,1024]{2,0,1:T(8,128)(2,1)} %bitcast.43), calls=%async_computation | async-start | bytes 4194304 | tf_op jit(solution)/shard_map/all_to_all | solution.py:49
  39.4 0.0 copy-done.3
  39.4 0.1 dynamic-slice_bitcast_fusion
  39.5 0.2 reduce_window_sum.34
  39.7 0.1 iota_add_fusion
  39.8 0.1 select_reduce_fusion.3
  39.9 0.1 ge.24
  40.0 47.6 %all-to-all-done = bf16[256,4,1024]{2,0,1:T(8,128)(2,1)S(1)} async-done(((bf16[256,4,1024]{2,0,1:T(8,128)(2,1)}), bf16[256,4,1024]{2,0,1:T(8,128)(2,1)S(1)}, u32[]{:S(2)}, u32[]{:S(2)}) %all-to-all-start) | async-done | bytes 2097184 | tf_op jit(solution)/shard_map/all_to_all | solution.py:49
  87.6 2.8 %gather_fusion = bf16[16,128,1024]{2,1,0:T(8,128)(2,1)} fusion(bf16[8,128,1024]{2,1,0:T(8,128)(2,1)S(1)} %bitcast.41, s32[1024]{0:T(1024)S(1)} %pad_clamp_fusion.2), kind=kCustom, calls=%fused_computation.2 | custom fusion | bytes 8388672 | tf_op jit(solution)/shard_map/gather | solution.py:87
  90.4 4.5 %broadcast_select_fusion = bf16[4,4,128,1024]{3,2,1,0:T(8,128)(2,1)} fusion(bf16[4,4,128,1024]{3,2,1,0:T(8,128)(2,1)} %bitcast.42, pred[4,4]{1,0:T(4,128)(4,1)S(1)} %ge.24), kind=kLoop, calls=%fused_computation.12 | loop fusion | flops 2097152 | bytes 8388624 | tf_op jit(solution)/shard_map/jit(_where)/select_n | solution.py:85
  95.0 4.9 %all-to-all-start.1 = ((bf16[4,4,128,1024]{3,2,1,0:T(8,128)(2,1)}), bf16[4,4,128,1024]{3,2,1,0:T(8,128)(2,1)}, u32[]{:S(2)}, u32[]{:S(2)}) async-start(bf16[4,4,128,1024]{3,2,1,0:T(8,128)(2,1)} %broadcast_select_fusion), calls=%async_computation.1 | async-start | bytes 8388608 | tf_op jit(solution)/shard_map/all_to_all | solution.py:91
  99.9 0.6 broadcast.200
  100.5 0.7 reduce.3
  101.2 0.1 eq.87
  101.3 0.7 reduce_window_sum.35
  102.0 0.1 reshape.103
  102.1 0.1 fusion.15
  102.2 0.1 reduce_window_sum.33
  102.2 0.0 copy-done
  102.3 0.2 select_reduce_fusion.1
  102.5 0.7 gather_fusion.2
  103.2 0.1 select_reduce_fusion
  103.3 0.7 gather_fusion.3
  104.1 0.1 broadcast_bitcast_fusion
  104.1 43.9 %all-to-all-done.1 = bf16[4,4,128,1024]{3,2,1,0:T(8,128)(2,1)} async-done(((bf16[4,4,128,1024]{3,2,1,0:T(8,128)(2,1)}), bf16[4,4,128,1024]{3,2,1,0:T(8,128)(2,1)}, u32[]{:S(2)}, u32[]{:S(2)}) %all-to-all-start.1) | async-done | bytes 4194336 | tf_op jit(solution)/shard_map/all_to_all | solution.py:91
  148.1 7.1 %gather_fusion.1 = bf16[32,128,1024]{2,1,0:T(8,128)(2,1)} fusion(bf16[16,128,1024]{2,1,0:T(8,128)(2,1)} %bitcast.10, s32[1024]{0:T(1024)S(1)} %pad_clamp_fusion), kind=kCustom, calls=%fused_computation.3 | custom fusion | bytes 16777344 | tf_op jit(solution)/shard_map/gather | solution.py:99
  155.2 0.0 copy-start.4
  155.2 7.7 %fusion = f32[4096]{0:T(1024)S(1)} fusion(bf16[4096,1024]{1,0:T(8,128)(2,1)} %param.16, bf16[32,128,1024]{2,1,0:T(8,128)(2,1)} %gather_fusion.1, pred[4096]{0:T(1024)(128)(4,1)S(1)} %broadcast_bitcast_fusion), kind=kLoop, calls=%fused_computation.6 | loop fusion | flops 16773120 | bytes 16797696 | tf_op jit(solution)/shard_map/reduce_sum | solution.py:27
  162.9 35.3 %psum.7 = f32[4096]{0:T(1024)S(1)} all-reduce(f32[4096]{0:T(1024)S(1)} %fusion), channel_id=1, replica_groups=mesh['dp'=4,'seq'=4,'tensor'=2] {'seq','tensor'}, use_global_device_ids=true, to_apply=%region_11.13 | all-reduce | flops 4096 | bytes 32768 | tf_op jit(solution)/shard_map/psum | solution.py:104
  198.2 0.0 copy-done.4
  198.2 10.2 %fusion.2 = bf16[4096,1024]{1,0:T(8,128)(2,1)} fusion(f32[1024]{0:T(1024)S(1)} %copy-done.4, f32[4096]{0:T(1024)S(1)} %add_rsqrt_fusion, bf16[4096,1024]{1,0:T(8,128)(2,1)} %param.16, bf16[32,128,1024]{2,1,0:T(8,128)(2,1)} %gather_fusion.1, pred[4096]{0:T(1024)(128)(4,1)S(1)} %broadcast_bitcast_fusion), kind=kLoop, calls=%fused_computation.8 | loop fusion | flops 20971520 | bytes 25190400 | tf_op jit(solution)/shard_map/convert_element_type | solution.py:106
  (20 shorter events, 0.2 us)
Async XLA Ops:
  0.0 102.2 %copy-start = (s32[4,32]{1,0:T(4,128)S(1)}, s32[4,32]{1,0:T(4,128)}, u32[]{:S(2)}) copy-start(s32[4,32]{1,0:T(4,128)} %param.19) | copy-start | bytes 1540
  0.0 18.2 %copy-start.2 = (f32[4,1024]{1,0:T(4,128)S(1)}, f32[4,1024]{1,0:T(4,128)}, u32[]{:S(2)}) copy-start(f32[4,1024]{1,0:T(4,128)} %param.15) | copy-start | bytes 49156
  0.0 18.2 %copy-start.1 = (bf16[256,3200]{1,0:T(8,128)(2,1)S(1)}, bf16[256,3200]{1,0:T(8,128)(2,1)}, u32[]{:S(2)}) copy-start(bf16[256,3200]{1,0:T(8,128)(2,1)} %param.11) | copy-start | bytes 4915204
  0.0 19.1 %copy-start.5 = (f32[3200]{0:T(1024)S(1)}, f32[3200]{0:T(1024)}, u32[]{:S(2)}) copy-start(f32[3200]{0:T(1024)} %param.13) | copy-start | bytes 38404
  0.0 19.2 %copy-start.6 = (f32[3200]{0:T(1024)S(1)}, f32[3200]{0:T(1024)}, u32[]{:S(2)}) copy-start(f32[3200]{0:T(1024)} %param.12) | copy-start | bytes 38404
  31.5 7.9 %copy-start.3 = (s32[32,1]{0,1:T(1,128)S(1)}, s32[32,1]{0,1:T(1,128)}, u32[]{:S(2)}) copy-start(s32[32,1]{0,1:T(1,128)} %param.18) | copy-start | bytes 388
  33.0 54.6 %all-to-all-start = ((bf16[256,4,1024]{2,0,1:T(8,128)(2,1)}), bf16[256,4,1024]{2,0,1:T(8,128)(2,1)S(1)}, u32[]{:S(2)}, u32[]{:S(2)}) async-start(bf16[256,4,1024]{2,0,1:T(8,128)(2,1)} %bitcast.43), calls=%async_computation | async-start | bytes 4194304 | tf_op jit(solution)/shard_map/all_to_all | solution.py:49
  95.0 53.1 %all-to-all-start.1 = ((bf16[4,4,128,1024]{3,2,1,0:T(8,128)(2,1)}), bf16[4,4,128,1024]{3,2,1,0:T(8,128)(2,1)}, u32[]{:S(2)}, u32[]{:S(2)}) async-start(bf16[4,4,128,1024]{3,2,1,0:T(8,128)(2,1)} %broadcast_select_fusion), calls=%async_computation.1 | async-start | bytes 8388608 | tf_op jit(solution)/shard_map/all_to_all | solution.py:91
  155.2 43.0 %copy-start.4 = (f32[1024]{0:T(1024)S(1)}, f32[1024]{0:T(1024)}, u32[]{:S(2)}) copy-start(f32[1024]{0:T(1024)} %param.17) | copy-start | bytes 12292
where the time goes:
time: 209 us; the launch traced here: 208 us
  waiting for transfers between devices  91.6 us (44%)
  blocking collectives  35.3 us (17%)
  local copies, waits for them, and re-layouts  32.1 us (15%)
  other arithmetic  25.8 us (12%)
  matrix products  12.3 us (6%)
  starting transfers between devices  11.3 us (5%)
    all_to_all x1, waiting for transfers between devices, local(): lax.all_to_all(projected.reshape(local_rows, owners, column_block), 'seq'...  47.6 us
    all_to_all x1, waiting for transfers between devices, local(): lax.all_to_all(outgoing, 'dp', split_axis=0, concat_axis=0, tiled=True)  43.9 us
    psum x1, blocking collectives, local(): totals = lax.psum(squares, ('seq', 'tensor'))  35.3 us
    unnamed x17, local copies, waits for them, and re-layouts  18.8 us
    dot_general x1, matrix products, local(): jnp.dot(normed_in, weights_flat, preferred_element_type=jnp.float32)  12.3 us
    convert_element_type x1, other arithmetic, local(): (assembled.astype(jnp.float32) * scale[:, None] * norm_gain).astype(jnp.b...  10.2 us
    reduce_sum x1, other arithmetic, row_squares(): return jnp.sum(values * values, axis=-1)  7.74 us
    gather x1, local copies, waits for them, and re-layouts, local(): picked = incoming[jnp.clip(arrival_index, 0, replicas * capacity - 1)]  7.11 us
  transfers between devices with their start and end apart: 2, of which 2 were waited for; matrix products, arithmetic and copies ran while one was open for 2% of the time, Pallas kernels for 0%

commit v1 on v0

--- a/solution.py
+++ b/solution.py
@@ -46,12 +46,20 @@
         normed_in, weights_flat, preferred_element_type=jnp.float32
     ) + proj_bias.reshape(-1)
     projected = hidden.astype(jnp.bfloat16)
-    regrouped = lax.all_to_all(
-        projected.reshape(local_rows, owners, column_block),
-        "seq",
-        split_axis=1,
-        concat_axis=0,
-        tiled=True,
+    regrouped = jnp.concatenate(
+        lax.all_to_all(
+            jnp.stack(
+                jnp.split(
+                    projected.reshape(local_rows, owners, column_block),
+                    lax.axis_size("seq"),
+                    axis=1,
+                )
+            ),
+            "seq",
+            0,
+            0,
+        ),
+        axis=0,
     )
     group_rows = regrouped.reshape(owners * local_rows, column_block)
     destination = tile_dest[:, 0]

time: 209 us -> 217 us (1.038)
  local copies, waits for them, and re-layouts: 32.1 us -> 37.7 us
    split x0 -> x1, local copies, waits for them, and re-layouts: none -> 3.05 us  [local(): jnp.split(projected.reshape(local_rows, owners, column_block), lax.axis_s...]
where the time goes in v1:
time: 217 us
  waiting for transfers between devices  91.6 us (42%)
  local copies, waits for them, and re-layouts  37.7 us (17%)
  blocking collectives  35.3 us (16%)
  other arithmetic  27.3 us (13%)
  matrix products  13.3 us (6%)
  starting transfers between devices  11.3 us (5%)
    all_to_all x1, waiting for transfers between devices, local(): lax.all_to_all(jnp.stack(jnp.split(projected.reshape(local_rows, owners,...  47.6 us
    all_to_all x1, waiting for transfers between devices, local(): lax.all_to_all(outgoing, 'dp', split_axis=0, concat_axis=0, tiled=True)  43.9 us
    psum x1, blocking collectives, local(): totals = lax.psum(squares, ('seq', 'tensor'))  35.3 us
    unnamed x17, local copies, waits for them, and re-layouts  18.8 us
    dot_general x1, matrix products, local(): jnp.dot(normed_in, weights_flat, preferred_element_type=jnp.float32)  13.3 us
    convert_element_type x1, other arithmetic, local(): (assembled.astype(jnp.float32) * scale[:, None] * norm_gain).astype(jnp.b...  10.2 us
    reduce_sum x1, other arithmetic, row_squares(): return jnp.sum(values * values, axis=-1)  7.74 us
    gather x1, local copies, waits for them, and re-layouts, local(): picked = incoming[jnp.clip(arrival_index, 0, replicas * capacity - 1)]  7.11 us
  transfers between devices with their start and end apart: 2, of which 2 were waited for; matrix products, arithmetic and copies ran while one was open for 2% of the time, Pallas kernels for 0%

profile of v1, /device:TPU:0, one launch (start us, length us, event | category | flops | bytes accessed | tf_op | source)
XLA Modules:
  0.0 216.7 jit_solution(1969978950770498820)
XLA Ops:
  0.0 0.0 copy-start
  0.0 0.0 copy-start.2
  0.0 0.0 copy-start.1
  0.0 0.0 copy-start.6
  0.0 18.2 %copy.25 = bf16[400,8,4,1024]{3,1,2,0:T(8,128)(2,1)} copy(bf16[400,8,4,1024]{3,2,1,0:T(4,128)(2,1)} %bitcast.39) | data formatting | bytes 52428800
  18.2 0.0 copy-done.2
  18.2 0.0 copy-done.1
  18.3 0.3 convert_reduce_fusion
  18.6 0.6 fusion.6
  19.2 0.0 copy-done.5
  19.2 0.0 copy-done.6
  19.2 13.3 %fusion.3 = bf16[256,4096]{1,0:T(8,128)(2,1)} fusion(bf16[3200,4096]{1,0:T(8,128)(2,1)} %bitcast.40, f32[4096]{0:T(1024)S(1)} %bitcast.44, bf16[256,3200]{1,0:T(8,128)(2,1)S(1)} %copy-done.1, f32[3200]{0:T(1024)S(1)} %copy-done.5, f32[3200]{0:T(1024)S(1)} %copy-done.6, f32[256]{0:T(256)S(1)} %add_rsqrt_fusion.1, f32[256]{0:T(256)S(1)} %broadcast_multiply_fusion), kind=kOutput, calls=%fused_computation.11 | convolution fusion | flops 6717898752 | bytes 29993984 | tf_op jit(solution)/shard_map/dot_general | solution.py:45
  32.5 3.3 %reshape.100 = bf16[256,4,1024]{2,1,0:T(4,128)(2,1)S(1)} reshape(bf16[256,4096]{1,0:T(8,128)(2,1)} %fusion.3) | data formatting | bytes 4194304 | tf_op jit(solution)/shard_map/reshape | solution.py:53
  35.8 3.1 %fusion.20 = (bf16[256,1,1024]{2,1,0:T(2,128)(2,1)S(1)}, bf16[256,1,1024]{2,1,0:T(2,128)(2,1)S(1)}, bf16[256,1,1024]{2,1,0:T(2,128)(2,1)S(1)}, bf16[256,1,1024]{2,1,0:T(2,128)(2,1)S(1)}) fusion(bf16[256,4,1024]{2,1,0:T(4,128)(2,1)S(1)} %reshape.100), kind=kLoop, calls=%fused_computation.73 | loop fusion | bytes 4194304 | tf_op jit(solution)/shard_map/split | solution.py:52
  38.9 0.4 copy_bitcast_fusion
  39.2 0.4 copy_bitcast_fusion.2
  39.6 0.0 copy-start.3
  39.6 1.6 pad_maximum_fusion
  41.2 6.4 %all-to-all-start = ((bf16[4,256,1,1024]{3,1,2,0:T(8,128)(2,1)}), bf16[4,256,1,1024]{3,1,2,0:T(8,128)(2,1)S(1)}, u32[]{:S(2)}, u32[]{:S(2)}) async-start(bf16[4,256,1,1024]{3,1,2,0:T(8,128)(2,1)} %pad_maximum_fusion), calls=%async_computation | async-start | bytes 4194304 | tf_op jit(solution)/shard_map/all_to_all | solution.py:50
  47.6 0.0 copy-done.3
  47.6 0.1 dynamic-slice_bitcast_fusion
  47.7 0.2 reduce_window_sum.34
  47.9 0.1 iota_add_fusion
  47.9 0.1 select_reduce_fusion.3
  48.0 0.1 ge.24
  48.2 47.6 %all-to-all-done = bf16[4,256,1,1024]{3,1,2,0:T(8,128)(2,1)S(1)} async-done(((bf16[4,256,1,1024]{3,1,2,0:T(8,128)(2,1)}), bf16[4,256,1,1024]{3,1,2,0:T(8,128)(2,1)S(1)}, u32[]{:S(2)}, u32[]{:S(2)}) %all-to-all-start) | async-done | bytes 2097184 | tf_op jit(solution)/shard_map/all_to_all | solution.py:50
  95.8 2.8 %gather_fusion = bf16[16,128,1024]{2,1,0:T(8,128)(2,1)} fusion(bf16[8,128,1024]{2,1,0:T(8,128)(2,1)S(1)} %bitcast.41, s32[1024]{0:T(1024)S(1)} %pad_clamp_fusion.2), kind=kCustom, calls=%fused_computation.2 | custom fusion | bytes 8388672 | tf_op jit(solution)/shard_map/gather | solution.py:95
  98.6 4.5 %broadcast_select_fusion = bf16[4,4,128,1024]{3,2,1,0:T(8,128)(2,1)} fusion(bf16[4,4,128,1024]{3,2,1,0:T(8,128)(2,1)} %bitcast.42, pred[4,4]{1,0:T(4,128)(4,1)S(1)} %ge.24), kind=kLoop, calls=%fused_computation.12 | loop fusion | flops 2097152 | bytes 8388624 | tf_op jit(solution)/shard_map/jit(_where)/select_n | solution.py:93
  103.2 4.9 %all-to-all-start.1 = ((bf16[4,4,128,1024]{3,2,1,0:T(8,128)(2,1)}), bf16[4,4,128,1024]{3,2,1,0:T(8,128)(2,1)}, u32[]{:S(2)}, u32[]{:S(2)}) async-start(bf16[4,4,128,1024]{3,2,1,0:T(8,128)(2,1)} %broadcast_select_fusion), calls=%async_computation.1 | async-start | bytes 8388608 | tf_op jit(solution)/shard_map/all_to_all | solution.py:99
  108.1 0.6 broadcast.200
  108.7 0.7 reduce.3
  109.4 0.1 eq.87
  109.5 0.7 reduce_window_sum.35
  110.2 0.1 reshape.102
  110.3 0.1 fusion.15
  110.4 0.1 reduce_window_sum.33
  110.4 0.0 copy-done
  110.5 0.2 select_reduce_fusion.1
  110.7 0.7 gather_fusion.2
  111.4 0.1 select_reduce_fusion
  111.5 0.7 gather_fusion.3
  112.3 0.1 broadcast_bitcast_fusion
  112.3 43.9 %all-to-all-done.1 = bf16[4,4,128,1024]{3,2,1,0:T(8,128)(2,1)} async-done(((bf16[4,4,128,1024]{3,2,1,0:T(8,128)(2,1)}), bf16[4,4,128,1024]{3,2,1,0:T(8,128)(2,1)}, u32[]{:S(2)}, u32[]{:S(2)}) %all-to-all-start.1) | async-done | bytes 4194336 | tf_op jit(solution)/shard_map/all_to_all | solution.py:99
  156.3 7.1 %gather_fusion.1 = bf16[32,128,1024]{2,1,0:T(8,128)(2,1)} fusion(bf16[16,128,1024]{2,1,0:T(8,128)(2,1)} %bitcast.12, s32[1024]{0:T(1024)S(1)} %pad_clamp_fusion), kind=kCustom, calls=%fused_computation.3 | custom fusion | bytes 16777344 | tf_op jit(solution)/shard_map/gather | solution.py:107
  163.4 7.7 %fusion = f32[4096]{0:T(1024)S(1)} fusion(bf16[4096,1024]{1,0:T(8,128)(2,1)} %param.16, bf16[32,128,1024]{2,1,0:T(8,128)(2,1)} %gather_fusion.1, pred[4096]{0:T(1024)(128)(4,1)S(1)} %broadcast_bitcast_fusion), kind=kLoop, calls=%fused_computation.6 | loop fusion | flops 16773120 | bytes 16797696 | tf_op jit(solution)/shard_map/reduce_sum | solution.py:27
  171.1 35.3 %psum.7 = f32[4096]{0:T(1024)S(1)} all-reduce(f32[4096]{0:T(1024)S(1)} %fusion), channel_id=1, replica_groups=mesh['dp'=4,'seq'=4,'tensor'=2] {'seq','tensor'}, use_global_device_ids=true, to_apply=%region_11.13 | all-reduce | flops 4096 | bytes 32768 | tf_op jit(solution)/shard_map/psum | solution.py:112
  206.4 0.0 copy-done.4
  206.4 10.2 %fusion.2 = bf16[4096,1024]{1,0:T(8,128)(2,1)} fusion(f32[1024]{0:T(1024)S(1)} %copy-done.4, f32[4096]{0:T(1024)S(1)} %add_rsqrt_fusion, bf16[4096,1024]{1,0:T(8,128)(2,1)} %param.16, bf16[32,128,1024]{2,1,0:T(8,128)(2,1)} %gather_fusion.1, pred[4096]{0:T(1024)(128)(4,1)S(1)} %broadcast_bitcast_fusion), kind=kLoop, calls=%fused_computation.8 | loop fusion | flops 20971520 | bytes 25190400 | tf_op jit(solution)/shard_map/convert_element_type | solution.py:114
  (22 shorter events, 0.2 us)
Async XLA Ops:
  0.0 110.4 %copy-start = (s32[4,32]{1,0:T(4,128)S(1)}, s32[4,32]{1,0:T(4,128)}, u32[]{:S(2)}) copy-start(s32[4,32]{1,0:T(4,128)} %param.19) | copy-start | bytes 1540
  0.0 18.2 %copy-start.2 = (f32[4,1024]{1,0:T(4,128)S(1)}, f32[4,1024]{1,0:T(4,128)}, u32[]{:S(2)}) copy-start(f32[4,1024]{1,0:T(4,128)} %param.15) | copy-start | bytes 49156
  0.0 18.2 %copy-start.1 = (bf16[256,3200]{1,0:T(8,128)(2,1)S(1)}, bf16[256,3200]{1,0:T(8,128)(2,1)}, u32[]{:S(2)}) copy-start(bf16[256,3200]{1,0:T(8,128)(2,1)} %param.11) | copy-start | bytes 4915204
  0.0 19.1 %copy-start.5 = (f32[3200]{0:T(1024)S(1)}, f32[3200]{0:T(1024)}, u32[]{:S(2)}) copy-start(f32[3200]{0:T(1024)} %param.13) | copy-start | bytes 38404
  0.0 19.2 %copy-start.6 = (f32[3200]{0:T(1024)S(1)}, f32[3200]{0:T(1024)}, u32[]{:S(2)}) copy-start(f32[3200]{0:T(1024)} %param.12) | copy-start | bytes 38404
  39.6 8.0 %copy-start.3 = (s32[32,1]{0,1:T(1,128)S(1)}, s32[32,1]{0,1:T(1,128)}, u32[]{:S(2)}) copy-start(s32[32,1]{0,1:T(1,128)} %param.18) | copy-start | bytes 388
  41.2 54.6 %all-to-all-start = ((bf16[4,256,1,1024]{3,1,2,0:T(8,128)(2,1)}), bf16[4,256,1,1024]{3,1,2,0:T(8,128)(2,1)S(1)}, u32[]{:S(2)}, u32[]{:S(2)}) async-start(bf16[4,256,1,1024]{3,1,2,0:T(8,128)(2,1)} %pad_maximum_fusion), calls=%async_computation | async-start | bytes 4194304 | tf_op jit(solution)/shard_map/all_to_all | solution.py:50
  103.2 53.1 %all-to-all-start.1 = ((bf16[4,4,128,1024]{3,2,1,0:T(8,128)(2,1)}), bf16[4,4,128,1024]{3,2,1,0:T(8,128)(2,1)}, u32[]{:S(2)}, u32[]{:S(2)}) async-start(bf16[4,4,128,1024]{3,2,1,0:T(8,128)(2,1)} %broadcast_select_fusion), calls=%async_computation.1 | async-start | bytes 8388608 | tf_op jit(solution)/shard_map/all_to_all | solution.py:99
  163.4 43.0 %copy-start.4 = (f32[1024]{0:T(1024)S(1)}, f32[1024]{0:T(1024)}, u32[]{:S(2)}) copy-start(f32[1024]{0:T(1024)} %param.17) | copy-start | bytes 12292
